TPU v7x, 32 devices: a whole 2x2x4 slice. The times are simulated.
32 devices in a mesh: group: 4 (over y, x), fsdp: 2 (over core), tensor: 4 (over z).
Axes of the slice: x: 2, y: 2, z: 4, core: 2. Of those that a mesh axis runs over, the one named last changes fastest.
Arguments:
- patches: bfloat16 [4, 2, 8, 577, 1024], P('group', None, ('fsdp', 'tensor')), may hold values from -6 to 6
- output_grad: bfloat16 [4, 2, 8, 577, 1024], P('group', None, ('fsdp', 'tensor')), may hold values from -6 to 6
- live_counts: int32 [4, 2, 2], P('group'), may hold values from 1 to 4, as said below
- attn_master: float32 [4, 1024, 1024], P(None, 'fsdp', 'tensor')
- mlp_master: float32 [2, 1024, 4096], P(None, 'fsdp', 'tensor')
- vector_master: float32 [12, 1024], replicated
- attn_moments: float32 [4, 2, 4, 1024, 1024], P('group', None, None, 'fsdp', 'tensor'), as said below
- mlp_moments: float32 [4, 2, 2, 1024, 4096], P('group', None, None, 'fsdp', 'tensor'), as said below
- vector_moments: float32 [4, 2, 12, 1024], P('group'), as said below
- attn_outer: float32 [4, 1024, 1024], P(None, 'fsdp', 'tensor'), may hold values from -0.125 to 0.125
- mlp_outer: float32 [2, 1024, 4096], P(None, 'fsdp', 'tensor'), may hold values from -0.125 to 0.125
- vector_outer: float32 [12, 1024], replicated, may hold values from -0.625 to 0.625
Outputs:
- block_output: bfloat16 [4, 2, 8, 577, 1024], P('group', None, ('fsdp', 'tensor'))
- patches_grad: float32 [4, 2, 8, 577, 1024], P('group', None, ('fsdp', 'tensor'))
- attn_inner: float32 [4, 2, 4, 1024, 1024], P('group', None, None, 'fsdp', 'tensor')
- attn_state: float32 [3, 4, 1024, 1024], P(None, None, 'fsdp', 'tensor')
- attn_copy: bfloat16 [4, 1024, 1024], P(None, 'fsdp', 'tensor')
- mlp_inner: float32 [4, 2, 2, 1024, 4096], P('group', None, None, 'fsdp', 'tensor')
- mlp_state: float32 [3, 2, 1024, 4096], P(None, None, 'fsdp', 'tensor')
- mlp_copy: bfloat16 [2, 1024, 4096], P(None, 'fsdp', 'tensor')
- vector_inner: float32 [4, 2, 12, 1024], P('group')
- vector_state: float32 [3, 12, 1024], replicated
- vector_copy: bfloat16 [12, 1024], replicated
Inputs may be any that keep to these rules, and one draw needn't show every extreme that they name: live_counts[g, m, f] images are live, and they stand first, among the f-th block of 4 image slots of micro-batch m in group g; some entry equals 4. `attn_moments`: second moments are positive. `mlp_moments`: second moments are positive. `vector_moments`: second moments are positive.
All inputs are finite; a program needn't handle non-finite values.
Results may differ from a plain program's by a relative error of at most 0.012.
The roundings to bfloat16 on the way count: a program that leaves them out, or rounds other values in their place, can miss the bound.
Values may be sent and summed in bfloat16 or wider, within the bound.
A program may use at most 320 MiB of HBM per device.

v0:
```python
from functools import partial
import jax
import jax.numpy as jnp
from jax import lax
from jax.sharding import PartitionSpec as P

HD = 64
FF = 4096
STEP = 8
EPSILON = 1e-06
INNER_RATE = 0.02
VECTOR_RATE = 0.2
WEIGHT_DECAY = 0.1
OUTER_RATE = 0.7
OUTER_MOMENTUM = 0.9


def normalize(source, gain_row, shift_row):
    centre = source - jnp.mean(source, axis=-1, keepdims=True)
    spread = jnp.mean(centre * centre, axis=-1, keepdims=True)
    return centre * lax.rsqrt(spread + EPSILON) * gain_row + shift_row


def gelu_exact(source):
    return jax.nn.gelu(source, approximate=False)


def gelu_slope(source):
    return (
        0.5 * (1.0 + lax.erf(source * 0.7071067811865476))
        + source * jnp.exp(-0.5 * source * source) * 0.3989422804014327
    )


def inner_adamw(master, gradient, moments, step_rate, decay_rate):
    first_moment = 0.9 * moments[0] + 0.1 * gradient
    second_moment = 0.95 * moments[1] + 0.05 * gradient * gradient
    step_ratio = (
        first_moment / (1.0 - 0.9**STEP) / (jnp.sqrt(second_moment / (1.0 - 0.95**STEP)) + 1e-08)
    )
    return (master - step_rate * (step_ratio + decay_rate * master), second_moment)


def outer_nesterov(master, outer_old, difference):
    momentum = OUTER_MOMENTUM * outer_old + difference
    updated = master - OUTER_RATE * (difference + OUTER_MOMENTUM * momentum)
    return (jnp.stack([difference, momentum, updated]), updated.astype(jnp.bfloat16))


def attend_forward(score_scale, operands):
    queries_low, keys_low, values_low = operands
    scores = (
        jnp.einsum("qhe,khe->hqk", queries_low, keys_low, preferred_element_type=jnp.float32)
        * score_scale
    )
    highest = jnp.max(scores, axis=-1, keepdims=True)
    exponent = jnp.exp(scores - highest)
    totals = jnp.sum(exponent, axis=-1, keepdims=True)
    probs_low = (exponent / totals).astype(jnp.bfloat16)
    attended = jnp.einsum("hqk,khe->qhe", probs_low, values_low, preferred_element_type=jnp.float32)
    return (attended.astype(jnp.bfloat16), (highest + jnp.log(totals))[..., 0])


def attend_backward(score_scale, operands):
    queries_low, keys_low, values_low, log_totals, grad_attended = operands
    scores = (
        jnp.einsum("qhe,khe->hqk", queries_low, keys_low, preferred_element_type=jnp.float32)
        * score_scale
    )
    probs_full = jnp.exp(scores - log_totals[..., None])
    grad_probs = jnp.einsum(
        "qhe,khe->hqk", grad_attended, values_low, preferred_element_type=jnp.float32
    )
    grad_values = jnp.einsum(
        "hqk,qhe->khe",
        probs_full.astype(jnp.bfloat16),
        grad_attended,
        preferred_element_type=jnp.float32,
    )
    weighted = jnp.sum(probs_full * grad_probs, axis=-1, keepdims=True)
    grad_scores = (probs_full * (grad_probs - weighted)).astype(jnp.bfloat16)
    grad_queries = (
        jnp.einsum("hqk,khe->qhe", grad_scores, keys_low, preferred_element_type=jnp.float32)
        * score_scale
    )
    grad_keys = (
        jnp.einsum("hqk,qhe->khe", grad_scores, queries_low, preferred_element_type=jnp.float32)
        * score_scale
    )
    return (
        grad_queries.astype(jnp.bfloat16),
        grad_keys.astype(jnp.bfloat16),
        grad_values.astype(jnp.bfloat16),
    )


def local(
    patches,
    output_grad,
    live_counts,
    attn_master,
    mlp_master,
    vector_master,
    attn_moments,
    mlp_moments,
    vector_moments,
    attn_outer,
    mlp_outer,
    vector_outer,
):
    narrow = jnp.bfloat16
    single = jnp.float32
    tensor_index = lax.axis_index("tensor")
    fsdp_index = lax.axis_index("fsdp")
    micro_count = patches.shape[1]
    local_images = patches.shape[2]
    seq_len = patches.shape[3]
    width = patches.shape[4]
    head_cols = attn_master.shape[2]
    hidden_cols = mlp_master.shape[2]
    score_scale = HD ** (-0.5)
    attn_all, mlp_all = (
        lax.all_gather(attn_master.astype(narrow), "fsdp", axis=1, tiled=True),
        lax.all_gather(mlp_master.astype(narrow), "fsdp", axis=1, tiled=True),
    )
    bias_query = lax.dynamic_slice_in_dim(vector_master[4], tensor_index * head_cols, head_cols)
    bias_value = lax.dynamic_slice_in_dim(vector_master[5], tensor_index * head_cols, head_cols)
    head_width = attn_all.shape[2]
    heads_here = head_width // HD
    bias_hidden = lax.dynamic_slice_in_dim(
        vector_master[8:].reshape(-1), tensor_index * hidden_cols, hidden_cols
    )
    owner_counts = jnp.sum(
        jnp.where(jnp.arange(live_counts.shape[2]) == fsdp_index, live_counts[0], 0), axis=-1
    )
    slot_index = tensor_index * local_images + jnp.arange(local_images)
    alive_all = (slot_index[None, :] < owner_counts[:, None]).astype(single)
    forward_attend = partial(attend_forward, score_scale)
    backward_attend = partial(attend_backward, score_scale)
    qkv_acc = jnp.zeros((3, width, head_width), single)
    out_acc = jnp.zeros((width, head_width), single)
    fc_in_acc = jnp.zeros((width, hidden_cols), single)
    fc_out_acc = jnp.zeros((width, hidden_cols), single)
    hidden_bias_acc = jnp.zeros((hidden_cols,), single)
    query_bias_acc = jnp.zeros((head_width,), single)
    value_bias_acc = jnp.zeros((head_width,), single)
    vector_acc = jnp.zeros((6, width), single)
    outputs_mixed = []
    outputs_grad = []
    for batch_index in range(micro_count):
        inputs = patches[0, batch_index].astype(single)
        alive = alive_all[batch_index][:, None, None]
        normed_one = normalize(inputs, vector_master[0], vector_master[1]).astype(narrow)
        rows_attn = lax.all_gather(normed_one, "tensor", axis=0, tiled=True)
        image_count = rows_attn.shape[0]
        shape_heads = (image_count, seq_len, heads_here, HD)
        projected = jnp.einsum(
            "isd,jde->jise", rows_attn, attn_all[:3], preferred_element_type=single
        )
        queries_low = (projected[0] + bias_query).astype(narrow).reshape(shape_heads)
        keys_low = projected[1].astype(narrow).reshape(shape_heads)
        values_low = (projected[2] + bias_value).astype(narrow).reshape(shape_heads)
        attended, log_totals = lax.map(forward_attend, (queries_low, keys_low, values_low))
        attended = attended.reshape(image_count, seq_len, head_width)
        branch_one = lax.psum_scatter(
            jnp.einsum("ise,de->isd", attended, attn_all[3], preferred_element_type=single),
            "tensor",
            scatter_dimension=0,
            tiled=True,
        )
        resid_one = inputs + branch_one + vector_master[6]
        normed_two = normalize(resid_one, vector_master[2], vector_master[3]).astype(narrow)
        rows_mlp = lax.all_gather(normed_two, "tensor", axis=0, tiled=True)
        pre_act = (
            jnp.einsum("isd,df->isf", rows_mlp, mlp_all[0], preferred_element_type=single)
            + bias_hidden
        )
        hidden = gelu_exact(pre_act).astype(narrow)
        branch_two = lax.psum_scatter(
            jnp.einsum("isf,df->isd", hidden, mlp_all[1], preferred_element_type=single),
            "tensor",
            scatter_dimension=0,
            tiled=True,
        )
        outputs_mixed.append((alive * (resid_one + branch_two + vector_master[7])).astype(narrow))
        grad_out = alive * output_grad[0, batch_index].astype(single)
        rows_grad_two = lax.all_gather(grad_out.astype(narrow), "tensor", axis=0, tiled=True)
        fc_out_acc = fc_out_acc + jnp.einsum(
            "isd,isf->df", rows_grad_two, hidden, preferred_element_type=single
        )
        grad_hidden = jnp.einsum(
            "isd,df->isf", rows_grad_two, mlp_all[1], preferred_element_type=single
        )
        grad_pre = (grad_hidden * gelu_slope(pre_act)).astype(narrow)
        fc_in_acc = fc_in_acc + jnp.einsum(
            "isd,isf->df", rows_mlp, grad_pre, preferred_element_type=single
        )
        hidden_bias_acc = hidden_bias_acc + jnp.sum(grad_pre.astype(single), axis=(0, 1))
        grad_normed_two = lax.psum_scatter(
            jnp.einsum("isf,df->isd", grad_pre, mlp_all[0], preferred_element_type=single),
            "tensor",
            scatter_dimension=0,
            tiled=True,
        )
        unused_two, norm_pull_two = jax.vjp(
            normalize, resid_one, vector_master[2], vector_master[3]
        )
        back_resid, gain_two, shift_two = norm_pull_two(grad_normed_two)
        grad_resid = grad_out + back_resid
        rows_grad_one = lax.all_gather(grad_resid.astype(narrow), "tensor", axis=0, tiled=True)
        out_acc = out_acc + jnp.einsum(
            "isd,ise->de", rows_grad_one, attended, preferred_element_type=single
        )
        grad_attended = jnp.einsum(
            "isd,de->ise", rows_grad_one, attn_all[3], preferred_element_type=single
        ).astype(narrow)
        grad_queries, grad_keys, grad_values = lax.map(
            backward_attend,
            (queries_low, keys_low, values_low, log_totals, grad_attended.reshape(shape_heads)),
        )
        grad_queries = grad_queries.reshape(image_count, seq_len, head_width)
        grad_keys = grad_keys.reshape(image_count, seq_len, head_width)
        grad_values = grad_values.reshape(image_count, seq_len, head_width)
        grad_stack = jnp.stack([grad_queries, grad_keys, grad_values])
        qkv_acc = qkv_acc + jnp.einsum(
            "isd,jise->jde", rows_attn, grad_stack, preferred_element_type=single
        )
        query_bias_acc = query_bias_acc + jnp.sum(grad_queries.astype(single), axis=(0, 1))
        value_bias_acc = value_bias_acc + jnp.sum(grad_values.astype(single), axis=(0, 1))
        summed = jnp.einsum("ise,de->isd", grad_queries, attn_all[0], preferred_element_type=single)
        summed = summed + jnp.einsum(
            "ise,de->isd", grad_keys, attn_all[1], preferred_element_type=single
        )
        grad_normed_one = lax.psum_scatter(
            summed
            + jnp.einsum("ise,de->isd", grad_values, attn_all[2], preferred_element_type=single),
            "tensor",
            scatter_dimension=0,
            tiled=True,
        )
        unused_one, norm_pull_one = jax.vjp(normalize, inputs, vector_master[0], vector_master[1])
        back_inputs, gain_one, shift_one = norm_pull_one(grad_normed_one)
        outputs_grad.append(grad_resid + back_inputs)
        vector_acc = vector_acc + jnp.stack(
            [
                gain_one,
                shift_one,
                gain_two,
                shift_two,
                jnp.sum(grad_resid, axis=(0, 1)),
                jnp.sum(grad_out, axis=(0, 1)),
            ]
        )
    attn_grad_full = jnp.concatenate([qkv_acc, out_acc[None]], 0)
    query_row = lax.dynamic_update_slice_in_dim(
        jnp.zeros((width,), single), query_bias_acc, tensor_index * head_cols, 0
    )
    value_row = lax.dynamic_update_slice_in_dim(
        jnp.zeros((width,), single), value_bias_acc, tensor_index * head_cols, 0
    )
    mlp_grad_cols = jnp.stack([fc_in_acc, fc_out_acc])
    attn_grad, mlp_grad = (
        lax.psum_scatter(attn_grad_full, "fsdp", scatter_dimension=1, tiled=True),
        lax.psum_scatter(mlp_grad_cols, "fsdp", scatter_dimension=1, tiled=True),
    )
    hidden_rows = lax.dynamic_update_slice_in_dim(
        jnp.zeros((FF,), single), hidden_bias_acc, tensor_index * hidden_cols, 0
    ).reshape(-1, width)
    vector_part = jnp.concatenate(
        [vector_acc[:4], jnp.stack([query_row, value_row]), vector_acc[4:], hidden_rows], 0
    )
    vector_grad = lax.psum(vector_part, ("fsdp", "tensor"))
    new_attn, second_attn = inner_adamw(
        attn_master, attn_grad, attn_moments[0], INNER_RATE, WEIGHT_DECAY
    )
    new_mlp, second_mlp = inner_adamw(
        mlp_master, mlp_grad, mlp_moments[0], INNER_RATE, WEIGHT_DECAY
    )
    new_vector, second_vector = inner_adamw(
        vector_master, vector_grad, vector_moments[0], VECTOR_RATE, 0.0
    )
    diff_attn, diff_mlp, diff_vector = lax.psum(
        (attn_master - new_attn, mlp_master - new_mlp, vector_master - new_vector), "group"
    )
    groups = lax.axis_size("group")
    attn_state, attn_copy = outer_nesterov(attn_master, attn_outer, diff_attn / groups)
    mlp_state, mlp_copy = outer_nesterov(mlp_master, mlp_outer, diff_mlp / groups)
    vector_state, vector_copy = outer_nesterov(vector_master, vector_outer, diff_vector / groups)
    block_output = jnp.stack(outputs_mixed)[None]
    patches_grad = jnp.stack(outputs_grad)[None]
    attn_inner = jnp.stack([attn_grad, second_attn])[None]
    mlp_inner = jnp.stack([mlp_grad, second_mlp])[None]
    vector_inner = jnp.stack([vector_grad, second_vector])[None]
    return (
        block_output,
        patches_grad,
        attn_inner,
        attn_state,
        attn_copy,
        mlp_inner,
        mlp_state,
        mlp_copy,
        vector_inner,
        vector_state,
        vector_copy,
    )


def solution(mesh):
    placed = (
        P("group", None, ("fsdp", "tensor"), None, None),
        P("group", None, ("fsdp", "tensor"), None, None),
        P("group", None, None),
        P(None, "fsdp", "tensor"),
        P(None, "fsdp", "tensor"),
        P(),
        P("group", None, None, "fsdp", "tensor"),
        P("group", None, None, "fsdp", "tensor"),
        P("group", None, None, None),
        P(None, "fsdp", "tensor"),
        P(None, "fsdp", "tensor"),
        P(),
    )
    return jax.shard_map(
        local,
        mesh=mesh,
        in_specs=placed,
        out_specs=(
            P("group", None, ("fsdp", "tensor"), None, None),
            P("group", None, ("fsdp", "tensor"), None, None),
            P("group", None, None, "fsdp", "tensor"),
            P(None, None, "fsdp", "tensor"),
            P(None, "fsdp", "tensor"),
            P("group", None, None, "fsdp", "tensor"),
            P(None, None, "fsdp", "tensor"),
            P(None, "fsdp", "tensor"),
            P("group", None, None, None),
            P(),
            P(),
        ),
        check_vma=False,
    )
```

profile of v0, /device:TPU:0, one launch (start us, length us, event | category | flops | bytes accessed | tf_op | source)
XLA Modules:
  0.0 2521.2 jit_solution(1555532051777853854)
XLA Ops:
  23.5 93.8 %all-gather.19.cloned.1.call-done = bf16[4,577,1024]{2,1,0:T(8,128)(2,1)} async-done(((bf16[1,577,1024]{2,1,0:T(8,128)(2,1)}), bf16[4,577,1024]{2,1,0:T(8,128)(2,1)}) %all-gather.19.cloned.1.call-update) | async-done | bytes 4726800 | tf_op jit(solution)/shard_map/all_gather | solution.py:154
  126.6 81.9 %all-gather.11.cloned.1.call-done = bf16[4,577,1024]{2,1,0:T(8,128)(2,1)} async-done(((bf16[1,577,1024]{2,1,0:T(8,128)(2,1)}), bf16[4,577,1024]{2,1,0:T(8,128)(2,1)}) %all-gather.11.cloned.1.call-update) | async-done | bytes 4726800 | tf_op jit(solution)/shard_map/all_gather | solution.py:154
  240.4 25.3 %while.53 = (s32[]{:T(128)}, bf16[4,577,4,64]{1,3,2,0:T(8,128)(2,1)}, f32[4,4,577]{2,1,0:T(4,128)S(1)}, bf16[4,577,4,64]{1,3,2,0:T(8,128)(2,1)}, bf16[4,577,4,64...) while((s32[]{:T(128)}, bf16[4,577,4,64]{1,3,2,0:T(8,128)(2,1)}, ...), condition=%wide.region_16.17_spmd, body=%wide.region_13.16_spmd.sunk | while | flops 353050112 | bytes 17370320 | solution.py:163
  279.1 21.4 while.52
  312.4 122.7 %reduce-scatter.15.cloned.1.call-done = f32[1,577,1024]{2,1,0:T(8,128)} async-done(((f32[4,577,1024]{2,1,0:T(8,128)}), f32[1,577,1024]{2,1,0:T(8,128)}) %reduce-scatter.15.cloned.1.call-update) | async-done | bytes 2363408 | tf_op jit(solution)/shard_map/reduce_scatter | solution.py:165
  435.1 167.2 %reduce-scatter.11.cloned.1.call-done = f32[1,577,1024]{2,1,0:T(8,128)} async-done(((f32[4,577,1024]{2,1,0:T(8,128)}), f32[1,577,1024]{2,1,0:T(8,128)}) %reduce-scatter.11.cloned.1.call-update) | async-done | bytes 2363408 | tf_op jit(solution)/shard_map/reduce_scatter | solution.py:165
  629.3 83.4 %all-gather.21.cloned.1.call-done = bf16[4,577,1024]{2,1,0:T(8,128)(2,1)} async-done(((bf16[1,577,1024]{2,1,0:T(8,128)(2,1)}), bf16[4,577,1024]{2,1,0:T(8,128)(2,1)}) %all-gather.21.cloned.1.call-update) | async-done | bytes 4726800 | tf_op jit(solution)/shard_map/all_gather | solution.py:173
  712.7 10.2 fusion.225
  722.9 80.9 %all-gather.15.cloned.1.call-done = bf16[4,577,1024]{2,1,0:T(8,128)(2,1)} async-done(((bf16[1,577,1024]{2,1,0:T(8,128)(2,1)}), bf16[4,577,1024]{2,1,0:T(8,128)(2,1)}) %all-gather.15.cloned.1.call-update) | async-done | bytes 4726800 | tf_op jit(solution)/shard_map/all_gather | solution.py:173
  803.8 20.2 fusion.210
  824.0 70.3 %all-gather.23.cloned.1.call-done = bf16[4,577,1024]{2,1,0:T(8,128)(2,1)} async-done(((bf16[1,577,1024]{2,1,0:T(8,128)(2,1)}), bf16[4,577,1024]{2,1,0:T(8,128)(2,1)}) %all-gather.23.cloned.1.call-update) | async-done | bytes 4726800 | tf_op jit(solution)/shard_map/all_gather | solution.py:187
  894.3 12.3 convert_reduce_fusion.1
  917.0 67.8 %all-gather.27.cloned.1.call-done = bf16[4,577,1024]{2,1,0:T(8,128)(2,1)} async-done(((bf16[1,577,1024]{2,1,0:T(8,128)(2,1)}), bf16[4,577,1024]{2,1,0:T(8,128)(2,1)}) %all-gather.27.cloned.1.call-update) | async-done | bytes 4726800 | tf_op jit(solution)/shard_map/all_gather | solution.py:187
  984.7 12.5 convert_reduce_fusion
  1007.1 46.6 %fusion.116 = (bf16[4,577,1024]{2,1,0:T(8,128)(2,1)S(1)}, bf16[4,577,1024]{2,1,0:T(8,128)(2,1)}) fusion(f32[4,577,1024]{2,1,0:T(8,128)} %get-tuple-element.421, f32[1024]{0:T(1024)S(1)} %dynamic_slice.61, u8[577,1024]{1,0:T(8,128)(4,1)} %get-tuple-element.249, u8[577,1024]{1,0:T(8,128)(4,1)S(1)} %get-tuple-element.248, ...), kind=kLoop, calls=%fused_computation.127 | loop fusion | flops 333238272 | bytes 30728192 | tf_op jit(solution)/shard_map/convert_element_type | solution.py:178
  1063.8 10.6 fusion.227
  1074.5 74.4 %reduce-scatter.19.cloned.1.call-done = f32[1,577,1024]{2,1,0:T(8,128)} async-done(((f32[4,577,1024]{2,1,0:T(8,128)}), f32[1,577,1024]{2,1,0:T(8,128)}) %reduce-scatter.19.cloned.1.call-update) | async-done | bytes 2363408 | tf_op jit(solution)/shard_map/reduce_scatter | solution.py:199
  1148.9 166.6 %reduce-scatter.23.cloned.1.call-done = f32[1,577,1024]{2,1,0:T(8,128)} async-done(((f32[4,577,1024]{2,1,0:T(8,128)}), f32[1,577,1024]{2,1,0:T(8,128)}) %reduce-scatter.23.cloned.1.call-update) | async-done | bytes 2363408 | tf_op jit(solution)/shard_map/reduce_scatter | solution.py:199
  1320.8 161.4 %reduce-scatter.13.cloned.1.call-done = f32[1,577,1024]{2,1,0:T(8,128)} async-done(((f32[4,577,1024]{2,1,0:T(8,128)}), f32[1,577,1024]{2,1,0:T(8,128)}) %reduce-scatter.13.cloned.1.call-update) | async-done | bytes 2363408 | tf_op jit(solution)/shard_map/reduce_scatter | solution.py:179
  1482.1 167.2 %reduce-scatter.17.cloned.1.call-done = f32[1,577,1024]{2,1,0:T(8,128)} async-done(((f32[4,577,1024]{2,1,0:T(8,128)}), f32[1,577,1024]{2,1,0:T(8,128)}) %reduce-scatter.17.cloned.1.call-update) | async-done | bytes 2363408 | tf_op jit(solution)/shard_map/reduce_scatter | solution.py:179
  1700.8 51.3 %all-gather.29.cloned.1.call-done = bf16[4,577,1024]{2,1,0:T(8,128)(2,1)} async-done(((bf16[1,577,1024]{2,1,0:T(8,128)(2,1)}), bf16[4,577,1024]{2,1,0:T(8,128)(2,1)}) %all-gather.29.cloned.1.call-update) | async-done | bytes 4726800 | tf_op jit(solution)/shard_map/all_gather | solution.py:210
  1760.1 48.8 %while.55 = (s32[]{:T(128)}, bf16[4,577,4,64]{1,3,2,0:T(8,128)(2,1)S(1)}, bf16[4,577,4,64]{1,3,2,0:T(8,128)(2,1)}, bf16[4,577,4,64]{1,3,2,0:T(8,128)(2,1)}, bf16...) while((s32[]{:T(128)}, ...), condition=%wide.region_35.36_spmd, body=%wide.region_33.35_spmd.sunk | while | flops 869015040 | bytes 49660196 | solution.py:217
  1808.9 34.2 %all-gather.25.cloned.1.call-done = bf16[4,577,1024]{2,1,0:T(8,128)(2,1)} async-done(((bf16[1,577,1024]{2,1,0:T(8,128)(2,1)}), bf16[4,577,1024]{2,1,0:T(8,128)(2,1)}) %all-gather.25.cloned.1.call-update) | async-done | bytes 4726800 | tf_op jit(solution)/shard_map/all_gather | solution.py:210
  1858.7 53.2 %while.54 = (s32[]{:T(128)}, bf16[4,577,4,64]{1,3,2,0:T(8,128)(2,1)S(1)}, bf16[4,577,4,64]{1,3,2,0:T(8,128)(2,1)}, bf16[4,577,4,64]{1,3,2,0:T(8,128)(2,1)}, bf16...) while((s32[]{:T(128)}, ...), condition=%wide.region_26.27_spmd, body=%wide.region_24.26_spmd.sunk | while | flops 869015040 | bytes 49660196 | solution.py:217
  1952.0 9.5 fusion.183
  2025.6 79.9 %all-reduce.3.cloned.1.call-done = (f32[4,512,256]{1,2,0:T(8,128)}, f32[2,512,1024]{2,1,0:T(8,128)}) async-done(((f32[4,512,256]{1,2,0:T(8,128)}, f32[2,512,1024]{2,1,0:T(8,128)}), (f32[4,512,256]{1,2,0:T(8,128)}, f32[2,512,1024]{2,1,0:T(8,128)})) %all-reduce.3.cloned.1.call-update) | async-done | bytes 6291472 | tf_op jit(solution)/shard_map/psum | solution.py:282
  2120.4 13.2 fusion.262
  2133.6 12.4 pad_maximum_fusion
  2146.0 125.0 %reduce-scatter.21.cloned.1.call-done = f32[1,577,1024]{2,1,0:T(8,128)} async-done(((f32[4,577,1024]{2,1,0:T(8,128)}), f32[1,577,1024]{2,1,0:T(8,128)}) %reduce-scatter.21.cloned.1.call-update) | async-done | bytes 2363408 | tf_op jit(solution)/shard_map/reduce_scatter | solution.py:234
  2273.4 164.4 %reduce-scatter.25.cloned.1.call-done = f32[1,577,1024]{2,1,0:T(8,128)} async-done(((f32[4,577,1024]{2,1,0:T(8,128)}), f32[1,577,1024]{2,1,0:T(8,128)}) %reduce-scatter.25.cloned.1.call-update) | async-done | bytes 2363408 | tf_op jit(solution)/shard_map/reduce_scatter | solution.py:234
  2448.6 29.2 %psum.30 = f32[12,1024]{1,0:T(8,128)S(1)} all-reduce(f32[12,1024]{1,0:T(8,128)S(1)} %concatenate.7), channel_id=1, replica_groups=mesh['group'=4,'fsdp'=2,'tensor'=4] {'fsdp','tensor'}, use_global_device_ids=true, to_apply=%region_61.62 | all-reduce | flops 12288 | bytes 98304 | tf_op jit(solution)/shard_map/psum | solution.py:272
  2477.9 17.6 psum.31
  (482 shorter events, 518.1 us)
Async XLA Ops:
  7.2 16.3 all-gather.13.cloned.1.call-start
  10.1 107.3 %all-gather.19.cloned.1.call-start = ((), (), s32[]{:S(2)}) async-start(), calls=%async_computation.16 | async-start | bytes 5980160 | tf_op jit(solution)/shard_map/all_gather | solution.py:154
  19.3 189.2 %all-gather.11.cloned.1.call-start = ((), (), s32[]{:S(2)}) async-start(), calls=%async_computation.10 | async-start | bytes 5980160 | tf_op jit(solution)/shard_map/all_gather | solution.py:154
  20.0 415.1 %reduce-scatter.15.cloned.1.call-start = ((), (), s32[]{:S(2)}) async-start(), calls=%async_computation.17 | async-start | bytes 11960320 | tf_op jit(solution)/shard_map/reduce_scatter | solution.py:165
  273.1 329.1 %reduce-scatter.11.cloned.1.call-start = ((), (), s32[]{:S(2)}) async-start(), calls=%async_computation.12 | async-start | bytes 11960320 | tf_op jit(solution)/shard_map/reduce_scatter | solution.py:165
  308.4 293.9 %copy-start.65 = (f32[1,1024]{1,0:T(1,128)S(1)}, f32[1,1024]{1,0:T(1,128)}, u32[]{:S(2)}) copy-start(f32[1,1024]{1,0:T(1,128)} %get-tuple-element.393) | copy-start | bytes 12292
  308.4 320.9 %all-gather.17.cloned.1.call-start = ((), (), s32[]{:S(2)}) async-start(), calls=%async_computation.14 | async-start | bytes 6291456 | tf_op jit(solution)/shard_map/all_gather | solution.py:124
  312.3 400.3 %all-gather.21.cloned.1.call-start = ((), (), s32[]{:S(2)}) async-start(), calls=%async_computation.18 | async-start | bytes 5980160 | tf_op jit(solution)/shard_map/all_gather | solution.py:173
  609.2 194.6 %all-gather.15.cloned.1.call-start = ((), (), s32[]{:S(2)}) async-start(), calls=%async_computation.13 | async-start | bytes 5980160 | tf_op jit(solution)/shard_map/all_gather | solution.py:173
  609.9 284.4 %all-gather.23.cloned.1.call-start = ((), (), s32[]{:S(2)}) async-start(), calls=%async_computation.20 | async-start | bytes 5980160 | tf_op jit(solution)/shard_map/all_gather | solution.py:187
  623.7 361.1 %all-gather.27.cloned.1.call-start = ((), (), s32[]{:S(2)}) async-start(), calls=%async_computation.24 | async-start | bytes 5980160 | tf_op jit(solution)/shard_map/all_gather | solution.py:187
  628.2 520.7 %reduce-scatter.19.cloned.1.call-start = ((), (), s32[]{:S(2)}) async-start(), calls=%async_computation.21 | async-start | bytes 11960320 | tf_op jit(solution)/shard_map/reduce_scatter | solution.py:199
  916.9 398.6 %reduce-scatter.23.cloned.1.call-start = ((), (), s32[]{:S(2)}) async-start(), calls=%async_computation.25 | async-start | bytes 11960320 | tf_op jit(solution)/shard_map/reduce_scatter | solution.py:199
  1007.0 475.1 %reduce-scatter.13.cloned.1.call-start = ((), (), s32[]{:S(2)}) async-start(), calls=%async_computation.15 | async-start | bytes 11960320 | tf_op jit(solution)/shard_map/reduce_scatter | solution.py:179
  1063.8 585.5 %reduce-scatter.17.cloned.1.call-start = ((), (), s32[]{:S(2)}) async-start(), calls=%async_computation.19 | async-start | bytes 11960320 | tf_op jit(solution)/shard_map/reduce_scatter | solution.py:179
  1074.4 574.9 %copy-start.63 = (f32[1,1024]{1,0:T(1,128)S(1)}, f32[1,1024]{1,0:T(1,128)}, u32[]{:S(2)}) copy-start(f32[1,1024]{1,0:T(1,128)} %get-tuple-element.390) | copy-start | bytes 12292
  1074.4 677.7 %all-gather.29.cloned.1.call-start = ((), (), s32[]{:S(2)}) async-start(), calls=%async_computation.26 | async-start | bytes 5980160 | tf_op jit(solution)/shard_map/all_gather | solution.py:210
  1660.6 182.5 %all-gather.25.cloned.1.call-start = ((), (), s32[]{:S(2)}) async-start(), calls=%async_computation.22 | async-start | bytes 5980160 | tf_op jit(solution)/shard_map/all_gather | solution.py:210
  1665.2 286.8 %reduce-scatter.29.cloned.1.call-start = ((), (), s32[]{:S(2)}) async-start(), calls=%async_computation.29 | async-start | bytes 12582912 | tf_op jit(solution)/shard_map/reduce_scatter | solution.py:264
  1700.6 261.0 %reduce-scatter.27.cloned.1.call-start = ((), (), s32[]{:S(2)}) async-start(), calls=%async_computation.28 | async-start | bytes 6291456 | tf_op jit(solution)/shard_map/reduce_scatter | solution.py:263
  1937.4 168.1 %all-reduce.3.cloned.1.call-start = ((), (), s32[]{:S(2)}) async-start(), calls=%async_computation.30 | async-start | bytes 12582912 | tf_op jit(solution)/shard_map/psum | solution.py:282
  1968.6 302.4 %reduce-scatter.21.cloned.1.call-start = ((), (), s32[]{:S(2)}) async-start(), calls=%async_computation.23 | async-start | bytes 11960320 | tf_op jit(solution)/shard_map/reduce_scatter | solution.py:234
  1981.9 456.0 %reduce-scatter.25.cloned.1.call-start = ((), (), s32[]{:S(2)}) async-start(), calls=%async_computation.27 | async-start | bytes 11960320 | tf_op jit(solution)/shard_map/reduce_scatter | solution.py:234
  2133.6 137.4 %copy-start.4 = (bf16[1,1,1,577,1024]{4,3,2,1,0:T(8,128)(2,1)S(1)}, bf16[1,1,1,577,1024]{4,3,2,1,0:T(8,128)(2,1)}, u32[]{:S(2)}) copy-start(bf16[1,1,1,577,1024]{4,3,2,1,0:T(8,128)(2,1)} %copy-done.3) | copy-start | bytes 3545092
  2133.6 137.4 %copy-start.41 = (f32[1,1024]{1,0:T(1,128)S(1)}, f32[1,1024]{1,0:T(1,128)}, u32[]{:S(2)}) copy-start(f32[1,1024]{1,0:T(1,128)} %copy-done.40) | copy-start | bytes 12292
  2133.6 137.4 %copy-start.43 = (f32[577]{0:T(1024)S(1)}, f32[577]{0:T(1024)}, u32[]{:S(2)}) copy-start(f32[577]{0:T(1024)} %copy-done.42) | copy-start | bytes 6928
  2146.0 291.8 %copy-start.2 = (bf16[1,1,1,577,1024]{4,3,2,1,0:T(8,128)(2,1)S(1)}, bf16[1,1,1,577,1024]{4,3,2,1,0:T(8,128)(2,1)}, u32[]{:S(2)}) copy-start(bf16[1,1,1,577,1024]{4,3,2,1,0:T(8,128)(2,1)} %copy-done.1) | copy-start | bytes 3545092
  2146.0 291.8 %copy-start.39 = (f32[577]{0:T(1024)S(1)}, f32[577]{0:T(1024)}, u32[]{:S(2)}) copy-start(f32[577]{0:T(1024)} %copy-done.38) | copy-start | bytes 6928
  2146.0 291.8 %copy-start.49 = (f32[577]{0:T(1024)S(1)}, f32[577]{0:T(1024)}, u32[]{:S(2)}) copy-start(f32[577]{0:T(1024)} %copy-done.48) | copy-start | bytes 6928
  2273.4 168.6 %copy-start.52 = (f32[577]{0:T(1024)S(1)}, f32[577]{0:T(1024)}, u32[]{:S(2)}) copy-start(f32[577]{0:T(1024)} %copy-done.51) | copy-start | bytes 6928
  2273.4 168.7 %copy-start.47 = (f32[577]{0:T(1024)S(1)}, f32[577]{0:T(1024)}, u32[]{:S(2)}) copy-start(f32[577]{0:T(1024)} %copy-done.46) | copy-start | bytes 6928
  2273.4 168.7 %copy-start.58 = (f32[577]{0:T(1024)S(1)}, f32[577]{0:T(1024)}, u32[]{:S(2)}) copy-start(f32[577]{0:T(1024)} %copy-done.57) | copy-start | bytes 6928
  (86 other events, 780.0 us)
Sparse Core Ops, SparseCore 0:
  10.2 13.2 all-gather.12
  25.6 91.6 all-gather.18
  119.5 88.9 all-gather.10
  273.3 161.7 reduce-scatter.14
  438.0 164.2 reduce-scatter.10
  604.3 14.5 all-gather.16
  620.9 91.6 all-gather.20
  714.8 88.9 all-gather.14
  805.4 88.9 all-gather.22
  895.7 88.9 all-gather.26
  987.1 161.7 reduce-scatter.18
  1151.2 164.2 reduce-scatter.22
  1317.9 164.2 reduce-scatter.12
  1485.0 164.2 reduce-scatter.16
  1660.7 91.3 all-gather.28
  1754.1 88.9 all-gather.24
  1845.8 15.2 reduce-scatter.28
  1937.5 10.6 reduce-scatter.26
  1968.8 136.6 all-reduce.2
  2107.6 163.3 reduce-scatter.20
  2273.5 164.2 reduce-scatter.24
where the time goes:
time: 2530 us; the launch traced here: 2520 us
  waiting for transfers between devices  1800 us (71%)
  matrix products  322 us (13%)
  other arithmetic  213 us (8%)
  local copies, waits for them, and re-layouts  124 us (5%)
  blocking collectives  46.8 us (2%)
    reduce_scatter x2, waiting for transfers between devices, local(): lax.psum_scatter(jnp.einsum('isf,df->isd', hidden, mlp_all[1], preferred_...  329 us
    reduce_scatter x2, waiting for transfers between devices, local(): lax.psum_scatter(jnp.einsum('ise,de->isd', attended, attn_all[3], preferr...  290 us
    reduce_scatter x2, waiting for transfers between devices, local(): lax.psum_scatter(summed + jnp.einsum('ise,de->isd', grad_values, attn_all...  289 us
    reduce_scatter x2, waiting for transfers between devices, local(): lax.psum_scatter(jnp.einsum('isf,df->isd', grad_pre, mlp_all[0], preferre...  241 us
    all_gather x2, waiting for transfers between devices, local(): rows_attn = lax.all_gather(normed_one, 'tensor', axis=0, tiled=True)  176 us
    all_gather x2, waiting for transfers between devices, local(): rows_mlp = lax.all_gather(normed_two, 'tensor', axis=0, tiled=True)  164 us
    all_gather x2, waiting for transfers between devices, local(): lax.all_gather(grad_out.astype(narrow), 'tensor', axis=0, tiled=True)  138 us
    all_gather x2, waiting for transfers between devices, local(): lax.all_gather(grad_resid.astype(narrow), 'tensor', axis=0, tiled=True)  85.5 us
  transfers between devices with their start and end apart: 21, of which 18 were waited for; matrix products, arithmetic and copies ran while one was open for 21% of the time, Pallas kernels for 0%

commit v1 on v0

--- a/solution.py
+++ b/solution.py
@@ -13,6 +13,29 @@
 WEIGHT_DECAY = 0.1
 OUTER_RATE = 0.7
 OUTER_MOMENTUM = 0.9
+
+
+def joined_along(blocks, dim):
+    blocks = jnp.moveaxis(blocks, 0, dim)
+    shape = blocks.shape
+    return blocks.reshape(*shape[:dim], shape[dim] * shape[dim + 1], *shape[dim + 2 :])
+
+
+def doubled(x, axis):
+    devices, mine = (lax.axis_size(axis), lax.axis_index(axis))
+    blocks, apart = (x[None], 1)
+    while apart < devices:
+        partner_block = lax.ppermute(blocks, axis, [(i, i ^ apart) for i in range(devices)])
+        low = mine & apart == 0
+        blocks = jnp.concatenate(
+            [jnp.where(low, blocks, partner_block), jnp.where(low, partner_block, blocks)]
+        )
+        apart *= 2
+    return blocks
+
+
+def collect(x, axis, dim):
+    return joined_along(doubled(x, axis), dim)
 
 
 def normalize(source, gain_row, shift_row):
@@ -184,7 +207,7 @@
         )
         outputs_mixed.append((alive * (resid_one + branch_two + vector_master[7])).astype(narrow))
         grad_out = alive * output_grad[0, batch_index].astype(single)
-        rows_grad_two = lax.all_gather(grad_out.astype(narrow), "tensor", axis=0, tiled=True)
+        rows_grad_two = collect(grad_out.astype(narrow), "tensor", 0)
         fc_out_acc = fc_out_acc + jnp.einsum(
             "isd,isf->df", rows_grad_two, hidden, preferred_element_type=single
         )

time: 2530 us -> 2620 us (1.036)
  waiting for transfers between devices: 1800 us -> 1870 us
    ppermute x0 -> x4, waiting for transfers between devices: none -> 525 us  [doubled(): lax.ppermute(blocks, axis, [(i, i ^ apart) for i in range(devices)])]
    all_gather x2, waiting for transfers between devices: 164 us -> 0.01 us  [local(): rows_mlp = lax.all_gather(normed_two, 'tensor', axis=0, tiled=True)]
    reduce_scatter x2, waiting for transfers between devices: 241 us -> 94.8 us  [local(): lax.psum_scatter(jnp.einsum('isf,df->isd', grad_pre, mlp_all[0], preferre...]
    all_gather x2 -> x0, waiting for transfers between devices: 138 us -> none  [local(): lax.all_gather(grad_out.astype(narrow), 'tensor', axis=0, tiled=True)]
  transfers between devices with their start and end apart: 21 -> 23, of which waited for: 18 -> 17; matrix products, arithmetic and copies ran while one was open for 21% -> 21% of each run, Pallas kernels for 0% -> 0%
where the time goes in v1:
time: 2620 us; the launch traced here: 2610 us
  waiting for transfers between devices  1870 us (71%)
  matrix products  320 us (12%)
  other arithmetic  227 us (9%)
  local copies, waits for them, and re-layouts  129 us (5%)
  blocking collectives  46.8 us (2%)
    ppermute x4, waiting for transfers between devices, doubled(): lax.ppermute(blocks, axis, [(i, i ^ apart) for i in range(devices)])  525 us
    reduce_scatter x2, waiting for transfers between devices, local(): lax.psum_scatter(jnp.einsum('isf,df->isd', hidden, mlp_all[1], preferred_...  329 us
    reduce_scatter x2, waiting for transfers between devices, local(): lax.psum_scatter(jnp.einsum('ise,de->isd', attended, attn_all[3], preferr...  290 us
    reduce_scatter x2, waiting for transfers between devices, local(): lax.psum_scatter(summed + jnp.einsum('ise,de->isd', grad_values, attn_all...  290 us
    all_gather x2, waiting for transfers between devices, local(): rows_attn = lax.all_gather(normed_one, 'tensor', axis=0, tiled=True)  176 us
    reduce_scatter x2, waiting for transfers between devices, local(): lax.psum_scatter(jnp.einsum('isf,df->isd', grad_pre, mlp_all[0], preferre...  94.8 us
    all_gather x2, waiting for transfers between devices, local(): lax.all_gather(grad_resid.astype(narrow), 'tensor', axis=0, tiled=True)  83.2 us
    psum x1, waiting for transfers between devices, local(): lax.psum((attn_master - new_attn, mlp_master - new_mlp, vector_master - n...  79.8 us
  transfers between devices with their start and end apart: 23, of which 17 were waited for; matrix products, arithmetic and copies ran while one was open for 21% of the time, Pallas kernels for 0%

profile of v1, /device:TPU:0, one launch (start us, length us, event | category | flops | bytes accessed | tf_op | source)
XLA Modules:
  0.0 2614.9 jit_solution(1135461553674260278)
XLA Ops:
  23.5 93.8 %all-gather.17.cloned.1.call-done = bf16[4,577,1024]{2,1,0:T(8,128)(2,1)} async-done(((bf16[1,577,1024]{2,1,0:T(8,128)(2,1)}), bf16[4,577,1024]{2,1,0:T(8,128)(2,1)}) %all-gather.17.cloned.1.call-update) | async-done | bytes 4726800 | tf_op jit(solution)/shard_map/all_gather | solution.py:177
  126.6 81.9 %all-gather.9.cloned.1.call-done = bf16[4,577,1024]{2,1,0:T(8,128)(2,1)} async-done(((bf16[1,577,1024]{2,1,0:T(8,128)(2,1)}), bf16[4,577,1024]{2,1,0:T(8,128)(2,1)}) %all-gather.9.cloned.1.call-update) | async-done | bytes 4726800 | tf_op jit(solution)/shard_map/all_gather | solution.py:177
  240.4 25.3 while.53
  279.2 21.5 while.52
  312.6 122.5 %reduce-scatter.15.cloned.1.call-done = f32[1,577,1024]{2,1,0:T(8,128)} async-done(((f32[4,577,1024]{2,1,0:T(8,128)}), f32[1,577,1024]{2,1,0:T(8,128)}) %reduce-scatter.15.cloned.1.call-update) | async-done | bytes 2363408 | tf_op jit(solution)/shard_map/reduce_scatter | solution.py:188
  435.1 167.2 %reduce-scatter.11.cloned.1.call-done = f32[1,577,1024]{2,1,0:T(8,128)} async-done(((f32[4,577,1024]{2,1,0:T(8,128)}), f32[1,577,1024]{2,1,0:T(8,128)}) %reduce-scatter.11.cloned.1.call-update) | async-done | bytes 2363408 | tf_op jit(solution)/shard_map/reduce_scatter | solution.py:188
  626.1 66.2 %collective-permute-done = bf16[1,1,577,1024]{3,2,1,0:T(8,128)(2,1)} collective-permute-done((bf16[1,1,577,1024]{3,2,1,0:T(8,128)(2,1)}, bf16[1,1,577,1024]{3,2,1,0:T(8,128)(2,1)}, u32[]{:S(2)}, u32[]{:S(2)}) %collective-permute-start) | collective-permute-done | bytes 1181728 | tf_op jit(solution)/shard_map/ppermute | solution.py:28
  692.3 59.3 %collective-permute-done.2 = bf16[1,1,577,1024]{3,2,1,0:T(8,128)(2,1)} collective-permute-done((bf16[1,1,577,1024]{3,2,1,0:T(8,128)(2,1)}, bf16[1,1,577,1024]{3,2,1,0:T(8,128)(2,1)}, u32[]{:S(2)}, u32[]{:S(2)}) %collective-permute-start.2) | collective-permute-done | bytes 1181728 | tf_op jit(solution)/shard_map/ppermute | solution.py:28
  763.6 178.1 %collective-permute-done.3 = bf16[2,1,577,1024]{3,0,2,1:T(2,128)(2,1)} collective-permute-done((bf16[2,1,577,1024]{3,0,2,1:T(2,128)(2,1)}, bf16[2,1,577,1024]{3,0,2,1:T(2,128)(2,1)}, u32[]{:S(2)}, u32[]{:S(2)}) %collective-permute-start.3) | collective-permute-done | bytes 2363424 | tf_op jit(solution)/shard_map/ppermute | solution.py:28
  955.3 9.7 convert_reduce_fusion
  979.5 221.1 %collective-permute-done.1 = bf16[2,1,577,1024]{3,0,2,1:T(2,128)(2,1)S(1)} collective-permute-done((bf16[2,1,577,1024]{3,0,2,1:T(2,128)(2,1)S(1)}, bf16[2,1,577,1024]{3,0,2,1:T(2,128)(2,1)S(1)}, u32[]{:S(2)}, u32[]{:S(2)}) %collective-permute-start.1) | collective-permute-done | bytes 2363424 | tf_op jit(solution)/shard_map/ppermute | solution.py:28
  1203.8 19.4 fusion.214
  1223.2 14.0 convert_reduce_fusion.1
  1247.2 46.9 %fusion.116 = (bf16[4,577,1024]{2,1,0:T(8,128)(2,1)S(1)}, bf16[4,577,1024]{2,1,0:T(8,128)(2,1)}) fusion(f32[4,577,1024]{2,1,0:T(8,128)} %copy-done.28, f32[1024]{0:T(1024)S(1)} %dynamic_slice.61, u8[577,1024]{1,0:T(8,128)(4,1)} %get-tuple-element.249, u8[577,1024]{1,0:T(8,128)(4,1)S(1)} %get-tuple-element.248, u8[577,1024]{1,0:T(8,128)(4,1)} %get-tuple-element.266, ...), kind=kLoop, calls=%fused_computation.127 | loop fusion | flops 333238272 | bytes 30728192 | tf_op jit(solution)/shard_map/convert_element_type | solution.py:201
  1304.1 10.4 fusion.231
  1314.8 94.8 %reduce-scatter.19.cloned.1.call-done = f32[1,577,1024]{2,1,0:T(8,128)} async-done(((f32[4,577,1024]{2,1,0:T(8,128)}), f32[1,577,1024]{2,1,0:T(8,128)}) %reduce-scatter.19.cloned.1.call-update) | async-done | bytes 2363408 | tf_op jit(solution)/shard_map/reduce_scatter | solution.py:222
  1414.8 161.4 %reduce-scatter.13.cloned.1.call-done = f32[1,577,1024]{2,1,0:T(8,128)} async-done(((f32[4,577,1024]{2,1,0:T(8,128)}), f32[1,577,1024]{2,1,0:T(8,128)}) %reduce-scatter.13.cloned.1.call-update) | async-done | bytes 2363408 | tf_op jit(solution)/shard_map/reduce_scatter | solution.py:202
  1576.2 167.2 %reduce-scatter.17.cloned.1.call-done = f32[1,577,1024]{2,1,0:T(8,128)} async-done(((f32[4,577,1024]{2,1,0:T(8,128)}), f32[1,577,1024]{2,1,0:T(8,128)}) %reduce-scatter.17.cloned.1.call-update) | async-done | bytes 2363408 | tf_op jit(solution)/shard_map/reduce_scatter | solution.py:202
  1759.3 10.5 fusion.172
  1797.1 49.1 %all-gather.23.cloned.1.call-done = bf16[4,577,1024]{2,1,0:T(8,128)(2,1)} async-done(((bf16[1,577,1024]{2,1,0:T(8,128)(2,1)}), bf16[4,577,1024]{2,1,0:T(8,128)(2,1)}) %all-gather.23.cloned.1.call-update) | async-done | bytes 4726800 | tf_op jit(solution)/shard_map/all_gather | solution.py:233
  1854.4 48.7 %while.55 = (s32[]{:T(128)}, bf16[4,577,4,64]{1,3,2,0:T(8,128)(2,1)S(1)}, bf16[4,577,4,64]{1,3,2,0:T(8,128)(2,1)}, bf16[4,577,4,64]{1,3,2,0:T(8,128)(2,1)}, bf16...) while((s32[]{:T(128)}, ...), condition=%wide.region_35.36_spmd, body=%wide.region_33.35_spmd.sunk | while | flops 869015040 | bytes 49660196 | solution.py:240
  1903.1 34.1 %all-gather.21.cloned.1.call-done = bf16[4,577,1024]{2,1,0:T(8,128)(2,1)} async-done(((bf16[1,577,1024]{2,1,0:T(8,128)(2,1)}), bf16[4,577,1024]{2,1,0:T(8,128)(2,1)}) %all-gather.21.cloned.1.call-update) | async-done | bytes 4726800 | tf_op jit(solution)/shard_map/all_gather | solution.py:233
  1952.7 53.4 %while.54 = (s32[]{:T(128)}, bf16[4,577,4,64]{1,3,2,0:T(8,128)(2,1)S(1)}, bf16[4,577,4,64]{1,3,2,0:T(8,128)(2,1)}, bf16[4,577,4,64]{1,3,2,0:T(8,128)(2,1)}, bf16...) while((s32[]{:T(128)}, ...), condition=%wide.region_26.27_spmd, body=%wide.region_24.26_spmd.sunk | while | flops 869015040 | bytes 49660196 | solution.py:240
  2046.0 9.5 fusion.185
  2119.7 79.8 %all-reduce.3.cloned.1.call-done = (f32[4,512,256]{1,2,0:T(8,128)}, f32[2,512,1024]{2,1,0:T(8,128)}) async-done(((f32[4,512,256]{1,2,0:T(8,128)}, f32[2,512,1024]{2,1,0:T(8,128)}), (f32[4,512,256]{1,2,0:T(8,128)}, f32[2,512,1024]{2,1,0:T(8,128)})) %all-reduce.3.cloned.1.call-update) | async-done | bytes 6291472 | tf_op jit(solution)/shard_map/psum | solution.py:305
  2214.3 13.2 fusion.272
  2227.5 12.4 pad_maximum_fusion
  2239.9 125.3 %reduce-scatter.21.cloned.1.call-done = f32[1,577,1024]{2,1,0:T(8,128)} async-done(((f32[4,577,1024]{2,1,0:T(8,128)}), f32[1,577,1024]{2,1,0:T(8,128)}) %reduce-scatter.21.cloned.1.call-update) | async-done | bytes 2363408 | tf_op jit(solution)/shard_map/reduce_scatter | solution.py:257
  2367.5 164.4 %reduce-scatter.25.cloned.1.call-done = f32[1,577,1024]{2,1,0:T(8,128)} async-done(((f32[4,577,1024]{2,1,0:T(8,128)}), f32[1,577,1024]{2,1,0:T(8,128)}) %reduce-scatter.25.cloned.1.call-update) | async-done | bytes 2363408 | tf_op jit(solution)/shard_map/reduce_scatter | solution.py:257
  2542.6 29.2 %psum.30 = f32[12,1024]{1,0:T(8,128)S(1)} all-reduce(f32[12,1024]{1,0:T(8,128)S(1)} %concatenate.23), channel_id=1, replica_groups=mesh['group'=4,'fsdp'=2,'tensor'=4] {'fsdp','tensor'}, use_global_device_ids=true, to_apply=%region_61.62 | all-reduce | flops 12288 | bytes 98304 | tf_op jit(solution)/shard_map/psum | solution.py:295
  2571.9 17.6 psum.31
  2597.4 9.4 copy.185
  (515 shorter events, 530.2 us)
Async XLA Ops:
  7.2 16.3 all-gather.11.cloned.1.call-start
  10.1 107.3 %all-gather.17.cloned.1.call-start = ((), (), s32[]{:S(2)}) async-start(), calls=%async_computation.16 | async-start | bytes 5980160 | tf_op jit(solution)/shard_map/all_gather | solution.py:177
  18.8 189.7 %all-gather.9.cloned.1.call-start = ((), (), s32[]{:S(2)}) async-start(), calls=%async_computation.10 | async-start | bytes 5980160 | tf_op jit(solution)/shard_map/all_gather | solution.py:177
  19.5 415.6 %reduce-scatter.15.cloned.1.call-start = ((), (), s32[]{:S(2)}) async-start(), calls=%async_computation.17 | async-start | bytes 11960320 | tf_op jit(solution)/shard_map/reduce_scatter | solution.py:188
  273.1 329.1 %reduce-scatter.11.cloned.1.call-start = ((), (), s32[]{:S(2)}) async-start(), calls=%async_computation.12 | async-start | bytes 11960320 | tf_op jit(solution)/shard_map/reduce_scatter | solution.py:188
  308.6 293.7 %copy-start.76 = (f32[1,1024]{1,0:T(1,128)S(1)}, f32[1,1024]{1,0:T(1,128)}, u32[]{:S(2)}) copy-start(f32[1,1024]{1,0:T(1,128)} %get-tuple-element.401) | copy-start | bytes 12292
  308.6 638.6 %all-gather.15.cloned.1.call-start = ((), (), s32[]{:S(2)}) async-start(), calls=%async_computation.14 | async-start | bytes 6291456 | tf_op jit(solution)/shard_map/all_gather | solution.py:147
  312.5 634.7 %all-gather.19.cloned.1.call-start = ((), (), s32[]{:S(2)}) async-start(), calls=%async_computation.18 | async-start | bytes 5980160 | tf_op jit(solution)/shard_map/all_gather | solution.py:196
  609.7 594.1 %all-gather.13.cloned.1.call-start = ((), (), s32[]{:S(2)}) async-start(), calls=%async_computation.13 | async-start | bytes 5980160 | tf_op jit(solution)/shard_map/all_gather | solution.py:196
  621.2 71.2 %collective-permute-start = (bf16[1,1,577,1024]{3,2,1,0:T(8,128)(2,1)}, bf16[1,1,577,1024]{3,2,1,0:T(8,128)(2,1)}, u32[]{:S(2)}, u32[]{:S(2)}) collective-permute-start(bf16[1,1,577,1024]{3,2,1,0:T(8,128)(2,1)} %get-tuple-element.384), channel_id=1, source_target_pairs={{0,1},{1,0},{2,3},{3,2},{4,5},{5,4},{6,7},{7,6},{8,9},{9,8},{10,11... | collective-permute-start | bytes 3545096 | tf_op jit(solution)/shard_map/ppermute | solution.py:28
  625.3 126.3 %collective-permute-start.2 = (bf16[1,1,577,1024]{3,2,1,0:T(8,128)(2,1)}, bf16[1,1,577,1024]{3,2,1,0:T(8,128)(2,1)}, u32[]{:S(2)}, u32[]{:S(2)}) collective-permute-start(bf16[1,1,577,1024]{3,2,1,0:T(8,128)(2,1)} %get-tuple-element.382), channel_id=1, source_target_pairs={{0,1},{1,0},{2,3},{3,2},{4,5},{5,4},{6,7},{7,6},{8,9},{9,8},{10,11... | collective-permute-start | bytes 3545096 | tf_op jit(solution)/shard_map/ppermute | solution.py:28
  626.1 688.7 %reduce-scatter.23.cloned.1.call-start = ((), (), s32[]{:S(2)}) async-start(), calls=%async_computation.23 | async-start | bytes 11960320 | tf_op jit(solution)/shard_map/reduce_scatter | solution.py:222
  761.2 180.5 %collective-permute-start.3 = (bf16[2,1,577,1024]{3,0,2,1:T(2,128)(2,1)}, bf16[2,1,577,1024]{3,0,2,1:T(2,128)(2,1)}, u32[]{:S(2)}, u32[]{:S(2)}) collective-permute-start(bf16[2,1,577,1024]{3,0,2,1:T(2,128)(2,1)} %copy.157), channel_id=1, source_target_pairs={{0,2},{1,3},{2,0},{3,1},{4,6},{5,7},{6,4},{7,5},{8,10},{9,11},{10,... | collective-permute-start | bytes 7090184 | tf_op jit(solution)/shard_map/ppermute | solution.py:28
  975.1 434.5 %reduce-scatter.19.cloned.1.call-start = ((), (), s32[]{:S(2)}) async-start(), calls=%async_computation.20 | async-start | bytes 11960320 | tf_op jit(solution)/shard_map/reduce_scatter | solution.py:222
  977.0 223.6 %copy-start.21 = (bf16[1,1,577,1024]{3,2,1,0:T(8,128)(2,1)S(1)}, bf16[1,1,577,1024]{3,2,1,0:T(8,128)(2,1)}, u32[]{:S(2)}) copy-start(bf16[1,1,577,1024]{3,2,1,0:T(8,128)(2,1)} %get-tuple-element.438) | copy-start | bytes 3545092
  977.0 223.6 %copy-start.22 = (bf16[1,1,577,1024]{3,2,1,0:T(8,128)(2,1)S(1)}, bf16[1,1,577,1024]{3,2,1,0:T(8,128)(2,1)}, u32[]{:S(2)}) copy-start(bf16[1,1,577,1024]{3,2,1,0:T(8,128)(2,1)} %get-tuple-element.439) | copy-start | bytes 3545092
  979.4 221.2 %collective-permute-start.1 = (bf16[2,1,577,1024]{3,0,2,1:T(2,128)(2,1)S(1)}, bf16[2,1,577,1024]{3,0,2,1:T(2,128)(2,1)S(1)}, u32[]{:S(2)}, u32[]{:S(2)}) collective-permute-start(bf16[2,1,577,1024]{3,0,2,1:T(2,128)(2,1)S(1)} %copy.149), channel_id=1, source_target_pairs={{0,2},{1,3},{2,0},{3,1},{4,6},{5,7},{6,4},{7,5},{8,10},{9,11},{10,... | collective-permute-start | bytes 7090184 | tf_op jit(solution)/shard_map/ppermute | solution.py:28
  1247.2 329.0 %reduce-scatter.13.cloned.1.call-start = ((), (), s32[]{:S(2)}) async-start(), calls=%async_computation.15 | async-start | bytes 11960320 | tf_op jit(solution)/shard_map/reduce_scatter | solution.py:202
  1304.1 439.3 %reduce-scatter.17.cloned.1.call-start = ((), (), s32[]{:S(2)}) async-start(), calls=%async_computation.19 | async-start | bytes 11960320 | tf_op jit(solution)/shard_map/reduce_scatter | solution.py:202
  1314.5 428.8 %copy-start.74 = (f32[1,1024]{1,0:T(1,128)S(1)}, f32[1,1024]{1,0:T(1,128)}, u32[]{:S(2)}) copy-start(f32[1,1024]{1,0:T(1,128)} %get-tuple-element.398) | copy-start | bytes 12292
  1314.5 531.6 %all-gather.23.cloned.1.call-start = ((), (), s32[]{:S(2)}) async-start(), calls=%async_computation.24 | async-start | bytes 5980160 | tf_op jit(solution)/shard_map/all_gather | solution.py:233
  1754.7 182.5 %all-gather.21.cloned.1.call-start = ((), (), s32[]{:S(2)}) async-start(), calls=%async_computation.21 | async-start | bytes 5980160 | tf_op jit(solution)/shard_map/all_gather | solution.py:233
  1759.2 286.8 %reduce-scatter.29.cloned.1.call-start = ((), (), s32[]{:S(2)}) async-start(), calls=%async_computation.27 | async-start | bytes 12582912 | tf_op jit(solution)/shard_map/reduce_scatter | solution.py:287
  1797.0 258.5 %reduce-scatter.27.cloned.1.call-start = ((), (), s32[]{:S(2)}) async-start(), calls=%async_computation.26 | async-start | bytes 6291456 | tf_op jit(solution)/shard_map/reduce_scatter | solution.py:286
  2031.3 168.2 %all-reduce.3.cloned.1.call-start = ((), (), s32[]{:S(2)}) async-start(), calls=%async_computation.28 | async-start | bytes 12582912 | tf_op jit(solution)/shard_map/psum | solution.py:305
  2062.7 302.5 %reduce-scatter.21.cloned.1.call-start = ((), (), s32[]{:S(2)}) async-start(), calls=%async_computation.22 | async-start | bytes 11960320 | tf_op jit(solution)/shard_map/reduce_scatter | solution.py:257
  2075.9 456.0 %reduce-scatter.25.cloned.1.call-start = ((), (), s32[]{:S(2)}) async-start(), calls=%async_computation.25 | async-start | bytes 11960320 | tf_op jit(solution)/shard_map/reduce_scatter | solution.py:257
  2239.9 292.0 %copy-start.2 = (bf16[1,1,1,577,1024]{4,3,2,1,0:T(8,128)(2,1)S(1)}, bf16[1,1,1,577,1024]{4,3,2,1,0:T(8,128)(2,1)}, u32[]{:S(2)}) copy-start(bf16[1,1,1,577,1024]{4,3,2,1,0:T(8,128)(2,1)} %copy-done.1) | copy-start | bytes 3545092
  2239.9 292.0 %copy-start.50 = (f32[577]{0:T(1024)S(1)}, f32[577]{0:T(1024)}, u32[]{:S(2)}) copy-start(f32[577]{0:T(1024)} %copy-done.49) | copy-start | bytes 6928
  2239.9 292.0 %copy-start.60 = (f32[577]{0:T(1024)S(1)}, f32[577]{0:T(1024)}, u32[]{:S(2)}) copy-start(f32[577]{0:T(1024)} %copy-done.59) | copy-start | bytes 6928
  2367.4 168.7 %copy-start.58 = (f32[577]{0:T(1024)S(1)}, f32[577]{0:T(1024)}, u32[]{:S(2)}) copy-start(f32[577]{0:T(1024)} %copy-done.57) | copy-start | bytes 6928
  2367.5 168.7 %copy-start.69 = (f32[577]{0:T(1024)S(1)}, f32[577]{0:T(1024)}, u32[]{:S(2)}) copy-start(f32[577]{0:T(1024)} %copy-done.68) | copy-start | bytes 6928
  (100 other events, 1446.2 us)
Sparse Core Ops, SparseCore 0:
  10.2 13.2 all-gather.10
  25.6 91.6 all-gather.16
  119.5 88.9 all-gather.8
  273.2 161.7 reduce-scatter.14
  438.0 164.2 reduce-scatter.10
  604.2 14.5 all-gather.14
  620.9 130.0 all-gather.18
  753.1 178.3 all-gather.12
  975.2 255.0 reduce-scatter.22
  1247.3 162.2 reduce-scatter.18
  1411.9 164.2 reduce-scatter.12
  1579.1 164.2 reduce-scatter.16
  1754.8 91.3 all-gather.22
  1848.2 88.9 all-gather.20
  1939.9 15.2 reduce-scatter.28
  2031.4 10.6 reduce-scatter.26
  2062.8 136.6 all-reduce.2
  2201.7 163.3 reduce-scatter.20
  2367.6 164.2 reduce-scatter.24
